TPU v7x, 32 devices: a whole 2x2x4 slice. The times are simulated.
32 devices in a mesh: rep: 1, r: 8 (over y, z), s: 4 (over x, core).
Axes of the slice: x: 2, y: 2, z: 4, core: 2. Of those that a mesh axis runs over, the one named last changes fastest.
Arguments:
- x: bfloat16 [32, 4096, 512], P(('rep', 'r', 's'))
- dy: bfloat16 [32, 4096, 512], P(('rep', 'r', 's'))
- w_gate: bfloat16 [2, 512, 1280], P(None, 's')
- w_up: bfloat16 [2, 512, 1280], P(None, 's')
- w_down: bfloat16 [2, 1280, 512], P(None, 's')
Outputs:
- output 1: bfloat16 [32, 4096, 512], P(('rep', 'r', 's'))
- output 2: bfloat16 [2, 512, 1280], P('rep', 's')
- output 3: bfloat16 [2, 512, 1280], P('rep', 's')
- output 4: bfloat16 [2, 1280, 512], P('rep', 's')
All inputs are finite; a program needn't handle non-finite values.
Results may differ from a plain program's by a relative error of at most 0.018.
Values are sent between devices in bfloat16 or wider.
A program may use at most 2 GiB of HBM per device.

v0:
```python
import jax
import jax.numpy as jnp
from jax import lax
from jax.sharding import PartitionSpec as P

NAMES = ("w_gate", "w_up", "w_down")


def matmul(a, w):
    return jnp.dot(a, w, preferred_element_type=jnp.float32).astype(jnp.bfloat16)


def normed(h):
    wide = h.astype(jnp.float32)
    scale = lax.rsqrt(jnp.mean(wide**2, -1, keepdims=True) + 1e-6)
    return (wide * scale).astype(jnp.bfloat16)


def layer(h, w):
    a = normed(h)
    gate = jnp.dot(a, w["w_gate"], preferred_element_type=jnp.float32)
    up = jnp.dot(a, w["w_up"], preferred_element_type=jnp.float32)
    return h + matmul((jax.nn.silu(gate) * up).astype(jnp.bfloat16), w["w_down"])


def solution(mesh):
    def fetched(weights, number):
        return {name: lax.all_gather(w[number], "s", axis=0, tiled=True) for name, w in zip(NAMES, weights, strict=True)}

    def summed(term):
        return lax.psum(lax.psum_scatter(term, "s", scatter_dimension=0, tiled=True), "r")

    def step(x, dy, *weights):
        layers = weights[0].shape[0]
        h, inputs = x[0], []
        for number in range(layers):
            inputs.append(h)
            h = layer(h, fetched(weights, number))
        by_h, mine = dy[0], [None] * layers
        for number in reversed(range(layers)):
            _, back = jax.vjp(lambda w, h: layer(h, w), fetched(weights, number), inputs[number])
            by_w, by_h = back(by_h)
            mine[number] = [summed(by_w[name]) for name in NAMES]
        return (by_h[None], *(jnp.stack([mine[number][i] for number in range(layers)]) for i in range(3)))

    states, cut = P(("rep", "r", "s"), None, None), P(None, "s", None)
    return jax.shard_map(
        step,
        mesh=mesh,
        in_specs=(states, states) + (cut,) * 3,
        out_specs=(states,) + (P("rep", "s", None),) * 3,
        check_vma=False,
    )
```

profile of v0, /device:TPU:0, one launch (start us, length us, event | category | flops | bytes accessed | tf_op | source)
XLA Modules:
  0.0 468.0 jit_solution(3858071530506674444)
XLA Ops:
  7.2 1.9 fusion.66
  9.2 0.0 all-gather.15.cloned.1.call-start
  9.2 2.0 fusion.67
  11.2 0.0 all-gather.17.cloned.1.call-start
  11.3 2.0 fusion.68
  13.3 0.5 all-gather.21.cloned.1.call-update
  13.9 0.5 all-gather.23.cloned.1.call-update
  14.5 0.5 all-gather.19.cloned.1.call-update
  15.0 6.3 %copy.10 = bf16[1,4096,512]{1,2,0:T(8,128)(2,1)} copy(bf16[1,4096,512]{2,1,0:T(8,128)(2,1)} %param.5) | data formatting | bytes 8388608 | tf_op args[0]
  21.4 3.1 fusion.15
  24.4 0.6 copy-done.4
  25.1 6.4 %copy.9 = bf16[1,4096,512]{1,2,0:T(8,128)(2,1)} copy(bf16[1,4096,512]{2,1,0:T(8,128)(2,1)} %param.6) | data formatting | bytes 8388608 | tf_op args[1]
  31.4 11.9 %fusion.46 = f32[4096,1280]{1,0:T(8,128)} fusion(bf16[1,4096,512]{1,2,0:T(8,128)(2,1)} %copy.10, f32[4096]{0:T(1024)S(1)} %fusion.59, bf16[1,512,1280]{2,1,0:T(8,128)(2,1)} %all-gather.13.cloned.1.call-done), kind=kOutput, calls=%fused_computation.65 | convolution fusion | flops 5375000576 | bytes 26492928 | tf_op jit(solution)/shard_map/dot_general | solution.py:21
  43.3 7.1 %all-gather.15.cloned.1.call-done = bf16[1,512,1280]{2,1,0:T(8,128)(2,1)} async-done(((bf16[1,128,1280]{2,1,0:T(8,128)(2,1)}), bf16[1,512,1280]{2,1,0:T(8,128)(2,1)}) %all-gather.15.cloned.1.call-update) | async-done | bytes 1310736 | tf_op jit(solution)/shard_map/all_gather | solution.py:28
  50.4 19.2 %multiply_convert_fusion.1 = (bf16[4096,1280]{1,0:T(8,128)(2,1)}, f32[4096,1280]{1,0:T(8,128)}) fusion(f32[4096,1280]{1,0:T(8,128)} %fusion.46, bf16[1,512,1280]{2,1,0:T(8,128)(2,1)} %all-gather.15.cloned.1.call-done, bf16[1,4096,512]{1,2,0:T(8,128)(2,1)} %copy.10, f32[4096]{0:T(1024)S(1)} %fusion.59), kind=kOutput, calls=%fused_computation.13 | convolution fusion | flops 5406457856 | bytes 57950208 | tf_op jit(solution)/shard_map/dot_general | solution.py:22
  69.6 0.4 all-gather.17.cloned.1.call-done
  70.0 11.3 %fusion.18 = (f32[4096]{0:T(1024)S(1)}, bf16[4096,512]{0,1:T(8,128)(2,1)}) fusion(bf16[4096,1280]{1,0:T(8,128)(2,1)} %get-tuple-element.20, bf16[1,1280,512]{2,1,0:T(8,128)(2,1)} %all-gather.17.cloned.1.call-done, bf16[1,4096,512]{1,2,0:T(8,128)(2,1)} %copy.10), kind=kOutput, calls=%fused_computation.40 | convolution fusion | flops 5379190784 | bytes 20201472 | tf_op jit(solution)/shard_map/dot_general | solution.py:10
  81.3 8.1 %all-gather.21.cloned.1.call-done = bf16[1,1280,512]{2,1,0:T(8,128)(2,1)} async-done(((bf16[1,320,512]{2,1,0:T(8,128)(2,1)}), bf16[1,1280,512]{2,1,0:T(8,128)(2,1)}) %all-gather.21.cloned.1.call-update) | async-done | bytes 1310736 | tf_op jit(solution)/shard_map/all_gather | solution.py:28
  89.4 10.3 %convolution_convert_fusion.1 = bf16[4096,1280]{1,0:T(8,128)(2,1)} fusion(bf16[1,4096,512]{2,1,0:T(8,128)(2,1)} %param.6, bf16[1,1280,512]{2,1,0:T(8,128)(2,1)} %all-gather.21.cloned.1.call-done), kind=kOutput, calls=%fused_computation.17 | convolution fusion | flops 5373952000 | bytes 15990784 | tf_op jit(solution)/shard_map/transpose(jvp())/dot_general | solution.py:10
  99.6 9.7 %all-gather.23.cloned.1.call-done = bf16[1,512,1280]{2,1,0:T(8,128)(2,1)} async-done(((bf16[1,128,1280]{2,1,0:T(8,128)(2,1)}), bf16[1,512,1280]{2,1,0:T(8,128)(2,1)}) %all-gather.23.cloned.1.call-update) | async-done | bytes 1310736 | tf_op jit(solution)/shard_map/all_gather | solution.py:28
  109.3 12.0 %fusion.38 = f32[4096,1280]{1,0:T(8,128)} fusion(bf16[4096,512]{0,1:T(8,128)(2,1)} %get-tuple-element.23, f32[4096]{0:T(1024)S(1)} %fusion.60, bf16[1,512,1280]{2,1,0:T(8,128)(2,1)} %all-gather.23.cloned.1.call-done), kind=kOutput, calls=%fused_computation.62 | convolution fusion | flops 5375000576 | bytes 26492928 | tf_op jit(solution)/shard_map/jvp()/dot_general | solution.py:22
  121.3 8.0 %all-gather.19.cloned.1.call-done = bf16[1,512,1280]{2,1,0:T(8,128)(2,1)} async-done(((bf16[1,128,1280]{2,1,0:T(8,128)(2,1)}), bf16[1,512,1280]{2,1,0:T(8,128)(2,1)}) %all-gather.19.cloned.1.call-update) | async-done | bytes 1310736 | tf_op jit(solution)/shard_map/all_gather | solution.py:28
  129.3 28.8 %fusion.1 = (bf16[4096,1280]{1,0:T(8,128)(2,1)}, f32[4096,1280]{1,0:T(8,128)}) fusion(f32[4096,1280]{1,0:T(8,128)} %fusion.38, bf16[4096,1280]{1,0:T(8,128)(2,1)} %convolution_convert_fusion.1, bf16[1,512,1280]{2,1,0:T(8,128)(2,1)} %all-gather.19.cloned.1.call-done, bf16[4096,512]{0,1:T(8,128)(2,1)} %get-tuple-element.23, f32[4096]{0:T(1024)S(1)} %fusion.60), kind=kOutput, calls=%fused_computation.7 | convolution fusion | flops 5437915136 | bytes 68435968 | tf_op jit(solution)/shard_map/jvp()/dot_general | solution.py:21
  158.1 18.5 %fusion.31 = bf16[1280,512]{1,0:T(8,128)(2,1)} fusion(bf16[1,4096,512]{2,1,0:T(8,128)(2,1)} %param.6, f32[4096,1280]{1,0:T(8,128)} %fusion.38, f32[4096,1280]{1,0:T(8,128)} %get-tuple-element.25), kind=kOutput, calls=%fused_computation.56 | convolution fusion | flops 5400821760 | bytes 47448064 | tf_op jit(solution)/shard_map/transpose(jvp())/dot_general | solution.py:10
  176.7 0.0 reduce-scatter.9.cloned.1.call-start
  176.8 15.4 %fusion.22 = bf16[4096,512]{0,1:T(8,128)(2,1)} fusion(bf16[4096,1280]{1,0:T(8,128)(2,1)} %convolution_convert_fusion.1, bf16[1,512,1280]{2,1,0:T(8,128)(2,1)S(1)} %copy-done.13, f32[4096,1280]{1,0:T(8,128)} %get-tuple-element.25), kind=kOutput, calls=%fused_computation.45 | convolution fusion | flops 5402263552 | bytes 36962304 | tf_op jit(solution)/shard_map/transpose(jvp())/dot_general | solution.py:22
  192.2 12.7 %fusion.20 = (f32[4096]{0:T(1024)S(1)}, bf16[4096,512]{0,1:T(8,128)(2,1)}) fusion(bf16[4096,512]{0,1:T(8,128)(2,1)S(1)} %copy-done.3, bf16[4096,512]{0,1:T(8,128)(2,1)} %fusion.22, bf16[4096,1280]{1,0:T(8,128)(2,1)} %get-tuple-element.24, bf16[1,512,1280]{2,1,0:T(8,128)(2,1)S(1)} %copy-done.14), kind=kOutput, calls=%fused_computation.42 | convolution fusion | flops 5379190784 | bytes 24395776 | tf_op jit(solution)/shard_map/transpose(jvp())/dot_general | solution.py:21
  204.9 6.7 %convolution_convert_fusion.5 = bf16[512,1280]{1,0:T(8,128)(2,1)} fusion(bf16[4096,1280]{1,0:T(8,128)(2,1)S(1)} %copy-done.15, bf16[4096,512]{0,1:T(8,128)(2,1)S(1)} %copy-done.3, f32[4096]{0:T(1024)S(1)} %fusion.60), kind=kOutput, calls=%fused_computation.57 | convolution fusion | flops 5375000576 | bytes 16007168 | tf_op jit(solution)/shard_map/transpose(jvp())/dot_general | solution.py:21
  211.6 0.0 reduce-scatter.15.cloned.1.call-start
  211.7 6.2 %fusion.28 = bf16[4096,512]{0,1:T(8,128)(2,1)S(1)} fusion(bf16[4096,512]{0,1:T(8,128)(2,1)} %get-tuple-element.23, bf16[4096,512]{0,1:T(8,128)(2,1)} %get-tuple-element.27, bf16[1,4096,512]{1,2,0:T(8,128)(2,1)} %copy.9, f32[4096]{0:T(1024)S(1)} %multiply_multiply_fusion.1, f32[4096]{0:T(1024)S(1)} %fusion.60), kind=kLoop, calls=%fused_computation.53 | loop fusion | flops 14680064 | bytes 16809984 | tf_op jit(solution)/shard_map/transpose(jvp())/add_any | solution.py:14
  217.9 2.0 copy-done.1
  219.9 9.6 %convolution_convert_fusion.7 = bf16[1280,512]{1,0:T(8,128)(2,1)} fusion(bf16[4096,1280]{1,0:T(8,128)(2,1)} %get-tuple-element.20, bf16[4096,512]{0,1:T(8,128)(2,1)S(1)} %fusion.28), kind=kOutput, calls=%fused_computation.61 | convolution fusion | flops 5369364480 | bytes 15990784 | tf_op jit(solution)/shard_map/transpose(jvp())/dot_general | solution.py:10
  229.5 0.0 reduce-scatter.13.cloned.1.call-start
  229.6 16.3 %fusion.35 = bf16[512,1280]{1,0:T(8,128)(2,1)} fusion(bf16[4096,1280]{1,0:T(8,128)(2,1)} %convolution_convert_fusion.1, bf16[4096,512]{0,1:T(8,128)(2,1)} %get-tuple-element.23, f32[4096]{0:T(1024)S(1)} %fusion.60, f32[4096,1280]{1,0:T(8,128)} %get-tuple-element.25), kind=kOutput, calls=%fused_computation.60 | convolution fusion | flops 5407113216 | bytes 36978688 | tf_op jit(solution)/shard_map/transpose(jvp())/dot_general | solution.py:22
  246.0 0.0 reduce-scatter.7.cloned.1.call-start
  246.0 27.7 %fusion.3 = (bf16[4096,1280]{1,0:T(8,128)(2,1)}, bf16[4096,1280]{1,0:T(8,128)(2,1)}) fusion(f32[4096,1280]{1,0:T(8,128)} %fusion.46, f32[4096,1280]{1,0:T(8,128)} %get-tuple-element.21, bf16[4096,512]{0,1:T(8,128)(2,1)} %copy-done.1, bf16[1,1280,512]{2,1,0:T(8,128)(2,1)S(1)} %copy-done.12), kind=kOutput, calls=%fused_computation.9 | convolution fusion | flops 5436866560 | bytes 68419584 | tf_op jit(solution)/shard_map/transpose(jvp())/dot_general | solution.py:10
  273.8 11.2 %convolution_convert_fusion.6 = bf16[512,1280]{1,0:T(8,128)(2,1)} fusion(bf16[4096,1280]{1,0:T(8,128)(2,1)} %get-tuple-element.28, bf16[1,4096,512]{1,2,0:T(8,128)(2,1)} %copy.10, f32[4096]{0:T(1024)S(1)} %copy-done.9), kind=kOutput, calls=%fused_computation.58 | convolution fusion | flops 5375000576 | bytes 16007168 | tf_op jit(solution)/shard_map/transpose(jvp())/dot_general | solution.py:21
  285.0 0.0 reduce-scatter.11.cloned.1.call-start
  285.1 16.4 %fusion.34 = bf16[512,1280]{1,0:T(8,128)(2,1)} fusion(bf16[4096,1280]{1,0:T(8,128)(2,1)} %get-tuple-element.29, bf16[1,4096,512]{1,2,0:T(8,128)(2,1)} %copy.10, f32[4096]{0:T(1024)S(1)} %copy-done.9, f32[4096,1280]{1,0:T(8,128)} %fusion.46), kind=kOutput, calls=%fused_computation.59 | convolution fusion | flops 5407113216 | bytes 36978688 | tf_op jit(solution)/shard_map/transpose(jvp())/dot_general | solution.py:22
  301.6 15.7 %fusion.21 = bf16[4096,512]{0,1:T(8,128)(2,1)} fusion(bf16[4096,1280]{1,0:T(8,128)(2,1)} %get-tuple-element.29, bf16[1,512,1280]{2,1,0:T(8,128)(2,1)S(1)} %copy-done.11, f32[4096,1280]{1,0:T(8,128)} %fusion.46), kind=kOutput, calls=%fused_computation.44 | convolution fusion | flops 5402263552 | bytes 36962304 | tf_op jit(solution)/shard_map/transpose(jvp())/dot_general | solution.py:22
  317.3 7.3 %reduce-scatter.7.cloned.1.call-done = bf16[128,1280]{1,0:T(8,128)(2,1)} async-done(((bf16[512,1280]{1,0:T(8,128)(2,1)}), bf16[128,1280]{1,0:T(8,128)(2,1)}) %reduce-scatter.7.cloned.1.call-update) | async-done | bytes 327696 | tf_op jit(solution)/shard_map/reduce_scatter | solution.py:31
  324.6 28.7 %reduce-scatter.11.cloned.1.call-done = bf16[128,1280]{1,0:T(8,128)(2,1)} async-done(((bf16[512,1280]{1,0:T(8,128)(2,1)}), bf16[128,1280]{1,0:T(8,128)(2,1)}) %reduce-scatter.11.cloned.1.call-update) | async-done | bytes 327696 | tf_op jit(solution)/shard_map/reduce_scatter | solution.py:31
  353.4 11.7 %fusion.17 = (f32[4096]{0:T(1024)S(1)}, bf16[4096,512]{0,1:T(8,128)(2,1)S(1)}) fusion(bf16[1,4096,512]{1,2,0:T(8,128)(2,1)} %copy.10, bf16[4096,512]{0,1:T(8,128)(2,1)} %fusion.21, bf16[4096,1280]{1,0:T(8,128)(2,1)} %get-tuple-element.28, bf16[1,512,1280]{2,1,0:T(8,128)(2,1)S(1)} %copy-done.10), kind=kOutput, calls=%fused_computation.39 | convolution fusion | flops 5379190784 | bytes 24395776 | tf_op jit(solution)/shard_map/transpose(jvp())/dot_general | solution.py:21
  365.2 4.2 fusion.27
  369.4 6.4 %copy.11 = bf16[1,4096,512]{2,1,0:T(8,128)(2,1)} copy(bf16[1,4096,512]{1,2,0:T(8,128)(2,1)} %fusion.27) | data formatting | bytes 8388608
  375.8 80.8 %all-reduce.3.cloned.1.call-done = (bf16[1,128,1280]{2,1,0:T(8,128)(2,1)}, bf16[1,128,1280]{2,1,0:T(8,128)(2,1)}, bf16[1,128,1280]{2,1,0:T(8,128)(2,1)}, bf16[1,...) async-done(((bf16[1,128,1280]{2,1,0:T(8,128)(2,1)}, bf16[1,128,1280]{2,1,0:T(8,128)(2,1)}, bf16[1,128,1280]{2,1,0:T(8,128)(2,1)}, ...) | async-done | bytes 1966096 | tf_op jit(solution)/shard_map/psum | solution.py:31
  456.6 2.0 pad_maximum_fusion.2
  458.6 2.4 pad_maximum_fusion
  (55 shorter events, 0.5 us)
Async XLA Ops:
  7.2 24.3 %all-gather.13.cloned.1.call-start = ((), (), s32[]{:S(2)}) async-start(), calls=%async_computation.12 | async-start | bytes 1638400 | tf_op jit(solution)/shard_map/all_gather | solution.py:28
  9.2 41.2 %all-gather.15.cloned.1.call-start = ((), (), s32[]{:S(2)}) async-start(), calls=%async_computation.13 | async-start | bytes 1638400 | tf_op jit(solution)/shard_map/all_gather | solution.py:28
  11.2 58.7 %all-gather.17.cloned.1.call-start = ((), (), s32[]{:S(2)}) async-start(), calls=%async_computation.14 | async-start | bytes 1638400 | tf_op jit(solution)/shard_map/all_gather | solution.py:28
  13.2 76.1 %all-gather.21.cloned.1.call-start = ((), (), s32[]{:S(2)}) async-start(), calls=%async_computation.16 | async-start | bytes 1638400 | tf_op jit(solution)/shard_map/all_gather | solution.py:28
  13.8 95.5 %all-gather.23.cloned.1.call-start = ((), (), s32[]{:S(2)}) async-start(), calls=%async_computation.17 | async-start | bytes 1638400 | tf_op jit(solution)/shard_map/all_gather | solution.py:28
  14.4 114.9 %all-gather.19.cloned.1.call-start = ((), (), s32[]{:S(2)}) async-start(), calls=%async_computation.15 | async-start | bytes 1638400 | tf_op jit(solution)/shard_map/all_gather | solution.py:28
  15.0 302.2 %reduce-scatter.17.cloned.1.call-start = ((), (), s32[]{:S(2)}) async-start(), calls=%async_computation.11 | async-start | bytes 1638400 | tf_op jit(solution)/shard_map/reduce_scatter | solution.py:31
  24.4 0.6 copy-start.4
  25.1 25.3 %copy-start.8 = (f32[4096]{0:T(1024)}, f32[4096]{0:T(1024)S(1)}, u32[]{:S(2)}) copy-start(f32[4096]{0:T(1024)S(1)} %fusion.59) | copy-start | bytes 49156
  81.3 18.4 %copy-start.6 = (f32[4096]{0:T(1024)}, f32[4096]{0:T(1024)S(1)}, u32[]{:S(2)}) copy-start(f32[4096]{0:T(1024)S(1)} %get-tuple-element.22) | copy-start | bytes 49156
  158.1 18.6 %copy-start.13 = (bf16[1,512,1280]{2,1,0:T(8,128)(2,1)S(1)}, bf16[1,512,1280]{2,1,0:T(8,128)(2,1)}, u32[]{:S(2)}) copy-start(bf16[1,512,1280]{2,1,0:T(8,128)(2,1)} %all-gather.23.cloned.1.call-done) | copy-start | bytes 3932164
  176.7 15.5 %copy-start.14 = (bf16[1,512,1280]{2,1,0:T(8,128)(2,1)S(1)}, bf16[1,512,1280]{2,1,0:T(8,128)(2,1)}, u32[]{:S(2)}) copy-start(bf16[1,512,1280]{2,1,0:T(8,128)(2,1)} %all-gather.19.cloned.1.call-done) | copy-start | bytes 3932164
  176.7 140.5 %reduce-scatter.9.cloned.1.call-start = ((), (), s32[]{:S(2)}) async-start(), calls=%async_computation.7 | async-start | bytes 1638400 | tf_op jit(solution)/shard_map/reduce_scatter | solution.py:31
  176.8 15.4 %copy-start.3 = (bf16[4096,512]{0,1:T(8,128)(2,1)S(1)}, bf16[4096,512]{0,1:T(8,128)(2,1)}, u32[]{:S(2)}) copy-start(bf16[4096,512]{0,1:T(8,128)(2,1)} %get-tuple-element.23) | copy-start | bytes 12582916
  192.2 12.7 %copy-start.7 = (f32[4096]{0:T(1024)S(1)}, f32[4096]{0:T(1024)}, u32[]{:S(2)}) copy-start(f32[4096]{0:T(1024)} %copy-done.6) | copy-start | bytes 49156
  192.2 12.7 %copy-start.15 = (bf16[4096,1280]{1,0:T(8,128)(2,1)S(1)}, bf16[4096,1280]{1,0:T(8,128)(2,1)}, u32[]{:S(2)}) copy-start(bf16[4096,1280]{1,0:T(8,128)(2,1)} %get-tuple-element.24) | copy-start | bytes 31457284
  211.6 105.6 %reduce-scatter.15.cloned.1.call-start = ((), (), s32[]{:S(2)}) async-start(), calls=%async_computation.10 | async-start | bytes 1638400 | tf_op jit(solution)/shard_map/reduce_scatter | solution.py:31
  217.9 2.0 copy-start.1
  229.5 16.5 %copy-start.12 = (bf16[1,1280,512]{2,1,0:T(8,128)(2,1)S(1)}, bf16[1,1280,512]{2,1,0:T(8,128)(2,1)}, u32[]{:S(2)}) copy-start(bf16[1,1280,512]{2,1,0:T(8,128)(2,1)} %all-gather.17.cloned.1.call-done) | copy-start | bytes 3932164
  229.5 87.7 %reduce-scatter.13.cloned.1.call-start = ((), (), s32[]{:S(2)}) async-start(), calls=%async_computation.9 | async-start | bytes 1638400 | tf_op jit(solution)/shard_map/reduce_scatter | solution.py:31
  246.0 78.7 %reduce-scatter.7.cloned.1.call-start = ((), (), s32[]{:S(2)}) async-start(), calls=%async_computation.6 | async-start | bytes 1638400 | tf_op jit(solution)/shard_map/reduce_scatter | solution.py:31
  246.0 27.8 %copy-start.9 = (f32[4096]{0:T(1024)S(1)}, f32[4096]{0:T(1024)}, u32[]{:S(2)}) copy-start(f32[4096]{0:T(1024)} %copy-done.8) | copy-start | bytes 49156
  285.0 68.3 %reduce-scatter.11.cloned.1.call-start = ((), (), s32[]{:S(2)}) async-start(), calls=%async_computation.8 | async-start | bytes 1638400 | tf_op jit(solution)/shard_map/reduce_scatter | solution.py:31
  285.1 16.5 %copy-start.11 = (bf16[1,512,1280]{2,1,0:T(8,128)(2,1)S(1)}, bf16[1,512,1280]{2,1,0:T(8,128)(2,1)}, u32[]{:S(2)}) copy-start(bf16[1,512,1280]{2,1,0:T(8,128)(2,1)} %all-gather.15.cloned.1.call-done) | copy-start | bytes 3932164
  301.5 51.9 %copy-start.10 = (bf16[1,512,1280]{2,1,0:T(8,128)(2,1)S(1)}, bf16[1,512,1280]{2,1,0:T(8,128)(2,1)}, u32[]{:S(2)}) copy-start(bf16[1,512,1280]{2,1,0:T(8,128)(2,1)} %all-gather.13.cloned.1.call-done) | copy-start | bytes 3932164
  301.5 155.1 %all-reduce.3.cloned.1.call-start = ((), (), s32[]{:S(2)}) async-start(), calls=%async_computation.18 | async-start | bytes 3932160 | tf_op jit(solution)/shard_map/psum | solution.py:31
  353.4 11.7 %copy-start.5 = (f32[4096]{0:T(1024)S(1)}, f32[4096]{0:T(1024)}, u32[]{:S(2)}) copy-start(f32[4096]{0:T(1024)} %copy-done.4) | copy-start | bytes 49156
  353.4 11.8 %copy-start = (bf16[1,4096,512]{1,2,0:T(8,128)(2,1)S(1)}, bf16[1,4096,512]{1,2,0:T(8,128)(2,1)}, u32[]{:S(2)}) copy-start(bf16[1,4096,512]{1,2,0:T(8,128)(2,1)} %copy.10) | copy-start | bytes 12582916
  353.4 11.8 %copy-start.2 = (bf16[4096,512]{0,1:T(8,128)(2,1)S(1)}, bf16[4096,512]{0,1:T(8,128)(2,1)}, u32[]{:S(2)}) copy-start(bf16[4096,512]{0,1:T(8,128)(2,1)} %copy-done.1) | copy-start | bytes 12582916
Sparse Core Ops, SparseCore 0:
  10.1 20.6 all-gather.12
  32.4 17.9 all-gather.14
  52.0 17.9 all-gather.16
  71.4 17.9 all-gather.20
  91.3 17.9 all-gather.22
  111.3 17.9 all-gather.18
  176.8 26.3 reduce-scatter.16
  211.7 26.3 reduce-scatter.8
  240.6 26.3 reduce-scatter.14
  269.4 26.3 reduce-scatter.12
  298.3 26.3 reduce-scatter.6
  327.0 26.3 reduce-scatter.10
  357.6 98.9 all-reduce.2
where the time goes:
time: 477 us; the launch traced here: 468 us
  matrix products  255 us (53%)
  waiting for transfers between devices  152 us (32%)
  local copies, waits for them, and re-layouts  27.6 us (6%)
  other arithmetic  18 us (4%)
  between operations  14.6 us (3%)
    dot_general x6, matrix products, layer(): up = jnp.dot(a, w['w_up'], preferred_element_type=jnp.float32)  94.9 us
    dot_general x6, matrix products, layer(): gate = jnp.dot(a, w['w_gate'], preferred_element_type=jnp.float32)  83 us
    psum x1, waiting for transfers between devices, summed(): lax.psum(lax.psum_scatter(term, 's', scatter_dimension=0, tiled=True), 'r')  80.8 us
    dot_general x5, matrix products, matmul(): jnp.dot(a, w, preferred_element_type=jnp.float32).astype(jnp.bfloat16)  77.5 us
    reduce_scatter x6, waiting for transfers between devices, summed(): lax.psum_scatter(term, 's', scatter_dimension=0, tiled=True)  36.1 us
    all_gather x6, waiting for transfers between devices, fetched(): lax.all_gather(w[number], 's', axis=0, tiled=True)  33.2 us
    unnamed x35, local copies, waits for them, and re-layouts  21.7 us
  transfers between devices with their start and end apart: 13, of which 8 were waited for; matrix products, arithmetic and copies ran while one was open for 52% of the time, Pallas kernels for 0%

commit v1 on v0

v1 whole, which is shorter than its diff:
```python
import functools

import jax
import jax.numpy as jnp
from jax import lax
from jax.experimental import pallas as pl
from jax.experimental.pallas import tpu as pltpu
from jax.sharding import PartitionSpec as P

MESH = pl.DeviceIdType.MESH
BF, F32 = jnp.bfloat16, jnp.float32
LAYERS, D, FF = 2, 512, 1280
HALF = FF // 2
CHUNKS = HALF // 128
STEPS = LAYERS * CHUNKS


def nn(a, b):
    return jnp.dot(a, b, preferred_element_type=F32)


def nt(a, b):
    return lax.dot_general(a, b, (((1,), (1,)), ((), ())), preferred_element_type=F32)


def tn(a, b):
    return lax.dot_general(a, b, (((0,), (0,)), ((), ())), preferred_element_type=F32)


def scale_of(wide):
    return lax.rsqrt(jnp.mean(wide * wide, -1, keepdims=True) + 1e-6)


def gated(gate):
    sig = 0.5 * jnp.tanh(0.5 * gate) + 0.5
    return sig, gate * sig


def kernel(
    x_ref, dy_ref, wg_ref, wu_ref, wd_ref,
    dx_ref, og_ref, ou_ref, od_ref,
    WG, WU, WD, XH, A, G, DA, ACT, ACC, ACD, DGU, AC2, WC, WDC,
    S0, s0s, s0r, S1, s1s, s1r, S2, s2s, s2r, S3, s3s, s3r, fin, dnx,
    lsem, xsem, gss, grs, ss, rs, zs, zr, ags, agr, dns, dnr,
):
    r, s = lax.axis_index("r"), lax.axis_index("s")
    y, z = r // 4, r % 4
    xx, core = s // 2, s % 2
    tokens = XH.shape[0]
    tt = tokens // 4
    partner = {"s": 2 * xx + (1 - core)}
    xn = {"s": 2 * (1 - xx) + core}

    def place(dy_, dz_):
        return {"r": ((y + dy_) % 2) * 4 + (z + dz_) % 4}

    others = [(a, b) for a in range(2) for b in range(4) if (a, b) != (0, 0)]

    barrier = pltpu.get_barrier_semaphore()
    for dev in [partner, xn] + [place(*o) for o in others]:
        pl.semaphore_signal(barrier, inc=1, device_id=dev, device_id_type=MESH)
    pl.semaphore_wait(barrier, 2 + len(others))

    def remote(src, dst, send, recv, dev):
        return pltpu.make_async_remote_copy(src_ref=src, dst_ref=dst, send_sem=send, recv_sem=recv, device_id=dev, device_id_type=MESH)

    mats = [(wg_ref, WG, D // 4), (wu_ref, WU, D // 4), (wd_ref, WD, FF // 4)]
    far = 2 * (1 - xx) + core

    def rows(W, layer, start, n):
        return W.at[layer, pl.ds(pl.multiple_of(start, 32), n), :]

    def fetch(layer, m, kind):
        shard, W, n = mats[m]
        i, h = 3 * layer + m, n // 2
        if kind == "own":
            return pltpu.make_async_copy(shard.at[layer], rows(W, layer, n * s, n), lsem.at[i])
        if kind == "near":
            src, dst, row, dev = shard.at[layer], rows(W, layer, n * s, n), 0, partner
        elif kind == "across":
            src, dst, row, dev = shard.at[layer, pl.ds(pl.multiple_of(h * y, 32), h), :], rows(W, layer, n * s + h * y, h), 1, xn
        else:
            start = n * far + h * (1 - y if kind == "other_near" else y)
            src = dst = rows(W, layer, start, h)
            row, dev = {"to_y": (2, place(1, 0)), "mine_near": (3, partner), "other_near": (4, partner)}[kind]
        return remote(src, dst, gss.at[row, i], grs.at[row, i], dev)

    def begin(layer, m):
        for kind in ("across", "near", "own"):
            fetch(layer, m, kind).start()

    def pass_x(layer, m):
        fetch(layer, m, "across").wait_recv()
        fetch(layer, m, "to_y").start()
        fetch(layer, m, "mine_near").start()

    def pass_y(layer, m):
        fetch(layer, m, "to_y").wait_recv()
        fetch(layer, m, "other_near").start()

    def arrived(layer, m):
        fetch(layer, m, "own").wait()
        for kind in ("near", "mine_near", "other_near"):
            fetch(layer, m, kind).wait_recv()

    for m in range(3):
        begin(0, m)
    tile = [pl.ds(t * tt, tt) for t in range(4)]
    load_x = [pltpu.make_async_copy(x_ref.at[t, :], XH.at[t, :], xsem.at[i]) for i, t in enumerate(tile)]
    load_dy = pltpu.make_async_copy(dy_ref, G, xsem.at[4])
    for copy in load_x:
        copy.start()
    load_dy.start()
    for t in range(4):
        load_x[t].wait()
        wide = XH[tile[t], :].astype(F32)
        A[0, tile[t], :] = (wide * scale_of(wide)).astype(BF)
    for m in range(3):
        pass_x(0, m)
    for m in range(3):
        begin(1, m)
    for m in range(3):
        pass_y(0, m)
    arrived(0, 0)
    arrived(0, 1)

    def up_front(t):
        a = A[0, tile[t], :]
        for f in range(FF // 256):
            c = slice(256 * f, 256 * f + 256)
            gate, up = nn(a, WG[0, :, c]), nn(a, WU[0, :, c])
            ACT[t % 2, :, c] = (gated(gate)[1] * up).astype(BF)

    def down_back(t):
        out = nn(ACT[t % 2], WD[0]).astype(BF).astype(F32)
        h = (XH[tile[t], :].astype(F32) + out).astype(BF)
        XH[tile[t], :] = h
        wide = h.astype(F32)
        A[1, tile[t], :] = (wide * scale_of(wide)).astype(BF)

    up_front(0)
    arrived(0, 2)
    for t in range(3):
        up_front(t + 1)
        down_back(t)
        if t == 0:
            pass_x(1, 0)
            pass_x(1, 1)
        if t == 1:
            pass_x(1, 2)
            pass_y(1, 0)
            pass_y(1, 1)
        if t == 2:
            pass_y(1, 2)
    down_back(3)
    for m in range(3):
        arrived(1, m)
    for layer in range(2):
        for m in range(3):
            for kind in ("near", "across", "to_y", "mine_near", "other_near"):
                fetch(layer, m, kind).wait_send()
    load_dy.wait()

    def pair(k, j, dev, src, dst):
        return remote(src, dst, ss.at[j, k % 2], rs.at[j, k % 2], dev)

    def core_copy(k):
        return pair(k, 0, partner, s0s, s0r.at[k % 2])

    def x_copy(k):
        return pair(k, 1, xn, s1s, s1r.at[k % 2])

    def y_copy(k):
        return pair(k, 2, place(1, 0), s2s, s2r.at[k % 2])

    def lanes(n):
        return pl.ds(pl.multiple_of(128 * n, 128), 128)

    def z_copies(k):
        return [
            remote(s3s.at[:, lanes((z + j) % 4)], s3r.at[k % 2, j - 1], zs.at[k % 2, j - 1], zr.at[k % 2, j - 1], place(0, j)) for j in range(1, 4)
        ]

    def piece(k):
        return fin.at[k, pl.ds(pl.multiple_of(96 * y, 32), 96), lanes(z)]

    def all_copies(k):
        return [remote(piece(k), piece(k), ags.at[k, i], agr.at[k, i], place(*o)) for i, o in enumerate(others)]

    def send_core():
        for x_ in range(2):
            for q in range(2):
                for buf, who in ((s0s, 1 - core), (S0, core)):
                    gu = ACC[pl.ds(pl.multiple_of(256 * x_ + 128 * who + 64 * q, 64), 64), :]
                    dn = ACD[pl.ds(pl.multiple_of(128 * x_ + 64 * who + 32 * q, 32), 32), :]
                    buf[x_, 96 * q : 96 * q + 64, :] = gu.astype(buf.dtype)
                    buf[x_, 96 * q + 64 : 96 * q + 96, :] = dn.astype(buf.dtype)

    def after_core(k):
        core_copy(k).wait()
        s1s[...] = (S0[1 - xx] + s0r[k % 2, 1 - xx].astype(F32)).astype(BF)
        x_copy(k).start()
        S1[...] = S0[xx] + s0r[k % 2, xx].astype(F32)

    def after_x(k):
        x_copy(k).wait()
        give, keep = (pl.ds(pl.multiple_of(96 * h, 32), 96) for h in (1 - y, y))
        s2s[...] = (S1[give, :] + s1r[k % 2, give, :].astype(F32)).astype(BF)
        y_copy(k).start()
        S2[...] = S1[keep, :] + s1r[k % 2, keep, :].astype(F32)

    def after_y(k):
        y_copy(k).wait()
        S3[...] = S2[...] + s2r[k % 2].astype(F32)
        s3s[...] = S3[...].astype(BF)
        for copy in z_copies(k):
            copy.start()

    def after_z(k):
        for copy in z_copies(k):
            copy.wait()
        total = S3[:, lanes(z)]
        for j in range(3):
            total += s3r[k % 2, j].astype(F32)
        piece(k)[...] = total.astype(BF)
        for copy in all_copies(k):
            copy.start()

    def after_all(k):
        for copy in all_copies(k):
            copy.wait()

    def when(cond, f, k):
        pl.when(cond)(lambda: f(k))

    def at(t):
        return pl.ds(pl.multiple_of(t * tt, tt), tt)

    def into(t, layer):
        wide, by_a = XH[at(t), :].astype(F32), DA[at(t), :].astype(BF).astype(F32)
        scale = scale_of(wide)
        back = by_a * scale - wide * (scale * scale * scale * jnp.mean(by_a * wide, -1, keepdims=True))
        G[at(t), :] = (G[at(t), :].astype(F32) + back.astype(BF).astype(F32)).astype(BF)

    def step(k, carry):
        layer, c = 1 - k // CHUNKS, k % CHUNKS

        @pl.when(k == CHUNKS)
        def _():
            def one(t, carry):
                into(t, 1)
                return carry

            lax.fori_loop(0, 4, one, 0)
            for copy in load_x:
                copy.start()

        @pl.when(c == 0)
        def _():
            DA[...] = jnp.zeros_like(DA)

        lo, hi = lanes(c), lanes(c + CHUNKS)
        WC[:, 0:128], WC[:, 128:256] = WG[layer, :, lo], WG[layer, :, hi]
        WC[:, 256:384], WC[:, 384:512] = WU[layer, :, lo], WU[layer, :, hi]
        WDC[0:128, :], WDC[128:256, :] = WD[layer, lo, :], WD[layer, hi, :]
        ACC[...] = jnp.zeros_like(ACC)
        ACD[...] = jnp.zeros_like(ACD)

        def front(t):
            gu = nn(A[layer, tile[t], :], WC[...])
            gate, up = gu[:, 0:256], gu[:, 256:512]
            by_act = nt(G[tile[t], :], WDC[...]).astype(BF).astype(F32)
            sig, silu = gated(gate)
            AC2[t % 2] = (silu * up).astype(BF)
            DGU[t % 2, :, 0:256] = (by_act * up * (sig * (1.0 + (gate - silu)))).astype(BF)
            DGU[t % 2, :, 256:512] = (by_act * silu).astype(BF)

        def back(t):
            ACC[...] += tn(A[layer, tile[t], :], DGU[t % 2])
            ACD[...] += tn(AC2[t % 2], G[tile[t], :])
            DA[tile[t], :] += nt(DGU[t % 2], WC[...])

        front(0)
        front(1)
        back(0)
        when(k >= 1, after_core, k - 1)
        front(2)
        back(1)
        when(k >= 2, after_y, k - 2)
        when(k >= 3, after_all, k - 3)
        front(3)
        back(2)
        back(3)
        when(k >= 2, after_z, k - 2)
        when(k >= 1, after_x, k - 1)
        send_core()
        core_copy(k).start()
        return carry

    lax.fori_loop(0, STEPS, step, 0)

    last = STEPS - 1
    after_core(last)
    after_y(last - 1)
    for copy in load_x:
        copy.wait()
    store_dx = [pltpu.make_async_copy(G.at[t, :], dx_ref.at[t, :], xsem.at[i]) for i, t in enumerate(tile)]
    for t in range(2):
        into(t, 0)
        store_dx[t].start()
    after_z(last - 1)
    after_x(last)
    for t in range(2, 4):
        into(t, 0)
        store_dx[t].start()
    after_y(last)
    after_all(last - 2)
    after_all(last - 1)

    def down_copies(layer):
        first = (1 - layer) * CHUNKS + (CHUNKS - 2) * (1 - core)
        return [
            remote(fin.at[pl.ds(first, 2), 96 * q + 64 : 96 * q + 96, :], dnx.at[layer, :, 32 * q : 32 * q + 32, :], dns.at[layer, q], dnr.at[layer, q], partner)
            for q in range(2)
        ]

    def put_out(layer):
        base = (1 - layer) * CHUNKS
        for c in range(CHUNKS):
            for q in range(2):
                block = fin[base + c, 96 * q : 96 * q + 64, :]
                rows_ = slice(64 * q, 64 * q + 64)
                for n, (out, start) in enumerate(((og_ref, 0), (og_ref, HALF), (ou_ref, 0), (ou_ref, HALF))):
                    out[layer, rows_, start + 128 * c : start + 128 * c + 128] = block[:, 128 * n : 128 * n + 128]
        for n in range(3):
            for q in range(2):
                od_ref[layer, 128 * n + 32 * q : 128 * n + 32 * q + 32, :] = fin[base + n + 2 * core, 96 * q + 64 : 96 * q + 96, :]
        for n in range(2):
            od_ref[layer, 128 * n + 64 : 128 * n + 128, :] = dnx[layer, n]

    for copy in down_copies(1):
        copy.start()
    after_z(last)
    for copy in down_copies(1):
        copy.wait()
    put_out(1)
    after_all(last)
    for copy in down_copies(0):
        copy.start()
    for copy in down_copies(0):
        copy.wait()
    put_out(0)
    for copy in store_dx:
        copy.wait()


def solution(mesh):
    def step(x, dy, wg, wu, wd):
        tokens = x.shape[1]
        tt = tokens // 4
        hbm, vmem = pl.BlockSpec(memory_space=pl.ANY), pl.BlockSpec(memory_space=pltpu.VMEM)
        V, DMA = pltpu.VMEM, pltpu.SemaphoreType.DMA
        dx, *grads = pl.pallas_call(
            kernel,
            out_shape=[
                jax.ShapeDtypeStruct((tokens, D), BF),
                *(jax.ShapeDtypeStruct(w.shape, BF) for w in (wg, wu, wd)),
            ],
            in_specs=[hbm] * 5,
            out_specs=[hbm, vmem, vmem, vmem],
            scratch_shapes=[
                V((LAYERS, D, FF), BF), V((LAYERS, D, FF), BF), V((LAYERS, FF, D), BF),
                V((tokens, D), BF), V((LAYERS, tokens, D), BF), V((tokens, D), BF), V((tokens, D), F32),
                V((2, tt, FF), BF), V((D, 512), F32), V((256, D), F32), V((2, tt, 512), BF), V((2, tt, 256), BF),
                V((D, 512), BF), V((256, D), BF),
                V((2, 192, 512), F32), V((2, 192, 512), BF), V((2, 2, 192, 512), BF),
                V((192, 512), F32), V((192, 512), BF), V((2, 192, 512), BF),
                V((96, 512), F32), V((96, 512), BF), V((2, 96, 512), BF),
                V((96, 512), F32), V((96, 512), BF), V((2, 3, 96, 128), BF),
                V((STEPS, 192, 512), BF), V((LAYERS, 2, 64, 512), BF),
                DMA((6,)), DMA((5,)), DMA((5, 6)), DMA((5, 6)), DMA((3, 2)), DMA((3, 2)),
                DMA((2, 3)), DMA((2, 3)), DMA((STEPS, 7)), DMA((STEPS, 7)), DMA((2, 2)), DMA((2, 2)),
            ],
            compiler_params=pltpu.CompilerParams(collective_id=0, has_side_effects=True, vmem_limit_bytes=67_043_328),
        )(x[0], dy[0], wg, wu, wd)
        return (dx[None], *grads)

    states, cut = P(("rep", "r", "s"), None, None), P(None, "s", None)
    return jax.shard_map(
        step,
        mesh=mesh,
        in_specs=(states, states) + (cut,) * 3,
        out_specs=(states,) + (P("rep", "s", None),) * 3,
        check_vma=False,
    )
```

time: 477 us -> 195 us (0.41); the launches traced: 468 us -> 194 us
  matrix products: 255 us -> 0 us
  Pallas kernels: 0 us -> 187 us
  waiting for transfers between devices: 152 us -> 0 us
  local copies, waits for them, and re-layouts: 27.6 us -> 7.13 us
  other arithmetic: 18 us -> 0 us
  between operations: 14.6 us -> 0.67 us
    dot_general x17 -> x0, matrix products: 255 us -> none  [the longest x6 94.9 us: layer(): up = jnp.dot(a, w['w_up'], preferred_element_type=jnp.float32)]
    pallas_call x0 -> x1, Pallas kernels: none -> 187 us  [step(): pl.pallas_call(kernel, out_shape=[jax.ShapeDtypeStruct((tokens, D), BF),...]
    psum x1 -> x0, waiting for transfers between devices: 80.8 us -> none  [summed(): lax.psum(lax.psum_scatter(term, 's', scatter_dimension=0, tiled=True), 'r')]
    reduce_scatter x6 -> x0, waiting for transfers between devices: 36.1 us -> none  [summed(): lax.psum_scatter(term, 's', scatter_dimension=0, tiled=True)]
    all_gather x6 -> x0, waiting for transfers between devices: 33.2 us -> none  [fetched(): lax.all_gather(w[number], 's', axis=0, tiled=True)]
    unnamed x35 -> x10, local copies, waits for them, and re-layouts: 21.7 us -> 7.13 us
    add_any x1 -> x0, other arithmetic: 6.22 us -> none  [normed(): wide = h.astype(jnp.float32)]
    slice x3 -> x0, local copies, waits for them, and re-layouts: 5.86 us -> none  [fetched(): w[number]]
  transfers between devices with their start and end apart: 13 -> 0, of which waited for: 8 -> 0; matrix products, arithmetic and copies ran while one was open for 52% -> 0% of each run, Pallas kernels for 0% -> 0%
where the time goes in v1:
time: 195 us; the launch traced here: 194 us
  Pallas kernels  187 us (96%)
  local copies, waits for them, and re-layouts  7.13 us (4%)
    pallas_call x1, Pallas kernels, step(): pl.pallas_call(kernel, out_shape=[jax.ShapeDtypeStruct((tokens, D), BF),...  187 us
    unnamed x10, local copies, waits for them, and re-layouts  7.13 us

profile of v1, /device:TPU:0, one launch (start us, length us, event | category | flops | bytes accessed | tf_op | source)
XLA Modules:
  0.0 194.4 jit_solution(17818589399401076871)
XLA Ops:
  0.6 186.6 %shard_map.84 = (bf16[4096,512]{1,0:T(8,128)(2,1)}, bf16[2,128,1280]{2,1,0:T(8,128)(2,1)}, bf16[2,128,1280]{2,1,0:T(8,128)(2,1)}, bf16[2,320,512]{2,1,0:T(8,128)(2,1)}) custom-call(bf16[4096,512]{1,0:T(8,128)(2,1)} %bitcast.3, bf16[4096,512]{1,0:T(8,128)(2,1)} %bitcast.4, bf16[2,128,1280]{2,1,0:T(8,128)(2,1)} %wg_ref.1, bf16[2,128,1280]{2,1,0:T(8,128)(2,1)} %wu_ref.1, ...), custom_call_target="tpu_custom_call" | custom-call | tf_op jit(solution)/shard_map/pallas_call | solution.py:363
  187.2 0.0 copy-start.2
  187.2 0.0 copy-start.1
  187.3 0.0 copy-start
  187.3 4.6 %copy.13 = bf16[1,4096,512]{2,1,0:T(8,128)(2,1)} copy(bf16[1,4096,512]{2,1,0:T(8,128)(2,1)} %bitcast.5) | data formatting | bytes 8388608
  191.9 0.0 copy-done.2
  191.9 0.8 copy.14
  192.7 0.0 copy-done.1
  192.7 0.8 copy.15
  193.5 0.0 copy-done
  193.6 0.8 copy.16
Async XLA Ops:
  187.2 4.6 %copy-start.2 = (bf16[2,128,1280]{2,1,0:T(8,128)(2,1)S(1)}, bf16[2,128,1280]{2,1,0:T(8,128)(2,1)}, u32[]{:S(2)}) copy-start(bf16[2,128,1280]{2,1,0:T(8,128)(2,1)} %get-tuple-element.17) | copy-start | bytes 1966084
  187.2 5.5 %copy-start.1 = (bf16[2,128,1280]{2,1,0:T(8,128)(2,1)S(1)}, bf16[2,128,1280]{2,1,0:T(8,128)(2,1)}, u32[]{:S(2)}) copy-start(bf16[2,128,1280]{2,1,0:T(8,128)(2,1)} %get-tuple-element.18) | copy-start | bytes 1966084
  187.3 6.3 %copy-start = (bf16[2,320,512]{2,1,0:T(8,128)(2,1)S(1)}, bf16[2,320,512]{2,1,0:T(8,128)(2,1)}, u32[]{:S(2)}) copy-start(bf16[2,320,512]{2,1,0:T(8,128)(2,1)} %get-tuple-element.19) | copy-start | bytes 1966084

commit v2 on v1

v2 whole, which is shorter than its diff:
```python
import functools

import jax
import jax.numpy as jnp
from jax import lax
from jax.experimental import pallas as pl
from jax.experimental.pallas import tpu as pltpu
from jax.sharding import PartitionSpec as P

MESH = pl.DeviceIdType.MESH
BF, F32 = jnp.bfloat16, jnp.float32
LAYERS, D, FF = 2, 512, 1280
HALF = FF // 2
CHUNKS = HALF // 128
STEPS = LAYERS * CHUNKS


def nn(a, b):
    return jnp.dot(a, b, preferred_element_type=F32)


def nt(a, b):
    return lax.dot_general(a, b, (((1,), (1,)), ((), ())), preferred_element_type=F32)


def tn(a, b):
    return lax.dot_general(a, b, (((0,), (0,)), ((), ())), preferred_element_type=F32)


def scale_of(wide):
    return lax.rsqrt(jnp.mean(wide * wide, -1, keepdims=True) + 1e-6)


def gated(gate):
    sig = 0.5 * jnp.tanh(0.5 * gate) + 0.5
    return sig, gate * sig


def kernel(
    x_ref, dy_ref, wg_ref, wu_ref, wd_ref,
    dx_ref, og_ref, ou_ref, od_ref,
    W, WD, XH, A, G, DGU, ACC, ACD, AC2,
    S0, s0s, s0r, S1, s1s, s1r, S2, s2s, s2r, S3, s3s, s3r, fin, dnx,
    lsem, ldsem, xsem, asem, osem, gss, grs, ss, rs, zs, zr, azs, azr, ays, ayr, dns, dnr,
):
    r, s = lax.axis_index("r"), lax.axis_index("s")
    y, z = r // 4, r % 4
    xx, core = s // 2, s % 2
    tokens = XH.shape[0]
    tt = tokens // 4
    partner = {"s": 2 * xx + (1 - core)}
    xn = {"s": 2 * (1 - xx) + core}

    def place(dy_, dz_):
        return {"r": ((y + dy_) % 2) * 4 + (z + dz_) % 4}

    others = [(a, b) for a in range(2) for b in range(4) if (a, b) != (0, 0)]

    def lanes(n):
        return pl.ds(pl.multiple_of(128 * n, 128), 128)

    def some(start, n):
        return pl.ds(pl.multiple_of(start, 32), n)

    def remote(src, dst, send, recv, dev):
        return pltpu.make_async_remote_copy(src_ref=src, dst_ref=dst, send_sem=send, recv_sem=recv, device_id=dev, device_id_type=MESH)

    def local_gu(layer, c, n):
        shard, half = ((wg_ref, 0), (wg_ref, CHUNKS), (wu_ref, 0), (wu_ref, CHUNKS))[n]
        return pltpu.make_async_copy(shard.at[layer, :, lanes(c + half)], W.at[layer, c, some(128 * s, 128), 128 * n : 128 * n + 128], lsem.at[layer, c, n])

    def unit(who, layer, i):
        n = 5 * (who % 2) + i
        return 256 * (n // 2) + 128 * (who // 2) + 64 * (n % 2)

    def local_d(layer, i):
        return pltpu.make_async_copy(wd_ref.at[layer, 64 * i : 64 * i + 64, :], WD.at[layer, some(unit(s, layer, i), 64), :], ldsem.at[layer, i])

    tile = [pl.ds(t * tt, tt) for t in range(4)]
    load_x = [pltpu.make_async_copy(x_ref.at[t, :], XH.at[t, :], xsem.at[i]) for i, t in enumerate(tile)]
    load_dy = pltpu.make_async_copy(dy_ref, G, xsem.at[4])
    for c in range(CHUNKS):
        for n in range(4):
            local_gu(0, c, n).start()
    for copy in load_x:
        copy.start()
    for i in range(5):
        local_d(0, i).start()
    for c in range(CHUNKS):
        for n in range(4):
            local_gu(1, c, n).start()
    for i in range(5):
        local_d(1, i).start()
    load_dy.start()

    barrier = pltpu.get_barrier_semaphore()
    for dev in [partner, xn] + [place(*o) for o in others]:
        pl.semaphore_signal(barrier, inc=1, device_id=dev, device_id_type=MESH)
    pl.semaphore_wait(barrier, 2 + len(others))

    far = 2 * (1 - xx) + core
    KINDS = ("near", "across", "to_y", "mine_near", "other_near")

    def fetch(layer, p, kind):
        who = s if kind in ("near", "across") else far
        row = KINDS.index(kind)
        dev = (partner, xn, place(1, 0), partner, partner)[row]
        half = 1 - y if kind == "other_near" else y
        if isinstance(p, int) and p >= CHUNKS:
            start = unit(who, layer, p - CHUNKS)
            ref = WD.at[layer, some(start, 64) if kind == "near" else some(start + 32 * half, 32), :]
        else:
            ref = W.at[layer, p, some(128 * who, 128) if kind == "near" else some(128 * who + 64 * half, 64), :]
        return remote(ref, ref, gss.at[layer, row, p], grs.at[layer, row, p], dev)

    def begin(layer, p):
        if p >= CHUNKS:
            local_d(layer, p - CHUNKS).wait()
        else:
            for n in range(4):
                local_gu(layer, p, n).wait()
        fetch(layer, p, "across").start()
        fetch(layer, p, "near").start()

    def pass_x(layer, p):
        fetch(layer, p, "across").wait_recv()
        fetch(layer, p, "to_y").start()
        fetch(layer, p, "mine_near").start()

    def pass_y(layer, p):
        fetch(layer, p, "to_y").wait_recv()
        fetch(layer, p, "other_near").start()

    def arrived(layer, p):
        for kind in ("near", "mine_near", "other_near"):
            fetch(layer, p, kind).wait_recv()

    downs = range(CHUNKS, CHUNKS + 5)
    for p in range(CHUNKS + 5):
        begin(0, p)
    save_a = [pltpu.make_async_copy(A.at[t, :], dx_ref.at[t, :], asem.at[i]) for i, t in enumerate(tile)]
    for t in range(4):
        load_x[t].wait()
        wide = XH[tile[t], :].astype(F32)
        A[tile[t], :] = (wide * scale_of(wide)).astype(BF)
        save_a[t].start()

    pass_x(0, 0)
    pass_x(0, 1)
    pass_x(0, 2)
    pass_y(0, 0)

    def up_front(c, carry):
        @pl.when(c + 3 < CHUNKS)
        def _():
            pass_x(0, c + 3)

        @pl.when(c + 1 < CHUNKS)
        def _():
            pass_y(0, c + 1)

        @pl.when(c == 3)
        def _():
            for p in downs:
                pass_x(0, p)
            for p in downs:
                begin(1, p)

        @pl.when(c == 4)
        def _():
            for p in downs:
                pass_y(0, p)
            for p in range(CHUNKS):
                begin(1, p)

        arrived(0, c)
        for t in range(4):
            gu = nn(A[tile[t], :], W[0, c])
            gate, up = gu[:, 0:256], gu[:, 256:512]
            DGU[c // 2, tile[t], pl.ds(pl.multiple_of(256 * (c % 2), 256), 256)] = (gated(gate)[1] * up).astype(BF)
        return carry

    lax.fori_loop(0, CHUNKS, up_front, 0)
    for p in downs:
        arrived(0, p)
    for copy in save_a:
        copy.wait()

    def down_back(t):
        out = nn(DGU[0, tile[t], :], WD[0, 0:512, :]) + nn(DGU[1, tile[t], :], WD[0, 512:1024, :]) + nn(DGU[2, tile[t], 0:256], WD[0, 1024:1280, :])
        h = (XH[tile[t], :].astype(F32) + out.astype(BF).astype(F32)).astype(BF)
        XH[tile[t], :] = h
        wide = h.astype(F32)
        A[tile[t], :] = (wide * scale_of(wide)).astype(BF)

    down_back(0)
    down_back(1)
    down_back(2)
    for p in downs:
        pass_x(1, p)
    down_back(3)
    for p in range(3):
        pass_x(1, p)
    for p in downs:
        pass_y(1, p)
    pass_y(1, 0)
    for p in downs:
        arrived(1, p)
    load_dy.wait()

    def pair(k, j, dev, src, dst):
        return remote(src, dst, ss.at[j, k % 2], rs.at[j, k % 2], dev)

    def core_copy(k):
        return pair(k, 0, partner, s0s, s0r.at[k % 2])

    def x_copies(k):
        return [pair(k, 1 + i, xn, s1s.at[some(96 * h, 96), :], s1r.at[k % 2, some(96 * h, 96), :]) for i, h in enumerate((1 - y, y))]

    def y_copy(k):
        return pair(k, 3, place(1, 0), s2s, s2r.at[k % 2])

    def z_copies(k):
        return [
            remote(s3s.at[:, lanes((z + j) % 4)], s3r.at[k % 2, j - 1], zs.at[k % 2, j - 1], zr.at[k % 2, j - 1], place(0, j)) for j in range(1, 4)
        ]

    def piece(k, z_=z):
        return fin.at[k, some(96 * y, 96), lanes(z_)]

    def out_z(k):
        return [remote(piece(k), piece(k), azs.at[k % 4, j - 1], azr.at[k % 4, j - 1], place(0, j)) for j in range(1, 4)]

    def out_y(k):
        return [remote(piece(k, (z + j) % 4), piece(k, (z + j) % 4), ays.at[k % 4, j], ayr.at[k % 4, j], place(1, 0)) for j in range(4)]

    def send_core():
        for x_ in range(2):
            for q in range(2):
                for buf, who in ((s0s, 1 - core), (S0, core)):
                    gu = ACC[pl.ds(pl.multiple_of(256 * x_ + 128 * who + 64 * q, 64), 64), :]
                    dn = ACD[some(128 * x_ + 64 * who + 32 * q, 32), :]
                    buf[x_, 96 * q : 96 * q + 64, :] = gu.astype(buf.dtype)
                    buf[x_, 96 * q + 64 : 96 * q + 96, :] = dn.astype(buf.dtype)

    def after_core(k):
        core_copy(k).wait()
        for copy, h in zip(x_copies(k), (1 - y, y), strict=True):
            half = some(96 * h, 96)
            s1s[half, :] = (S0[1 - xx, half, :] + s0r[k % 2, 1 - xx, half, :].astype(F32)).astype(BF)
            copy.start()
        S1[...] = S0[xx] + s0r[k % 2, xx].astype(F32)

    def after_x(k):
        x_copies(k)[0].wait()
        give, keep = (some(96 * h, 96) for h in (1 - y, y))
        s2s[...] = (S1[give, :] + s1r[k % 2, give, :].astype(F32)).astype(BF)
        y_copy(k).start()
        x_copies(k)[1].wait()
        S2[...] = S1[keep, :] + s1r[k % 2, keep, :].astype(F32)

    def after_y(k):
        y_copy(k).wait()
        S3[...] = S2[...] + s2r[k % 2].astype(F32)
        s3s[...] = S3[...].astype(BF)
        for copy in z_copies(k):
            copy.start()

    def after_z(k):
        for copy in z_copies(k):
            copy.wait()
        total = S3[:, lanes(z)]
        for j in range(3):
            total += s3r[k % 2, j].astype(F32)
        piece(k)[...] = total.astype(BF)
        for copy in (*out_z(k), out_y(k)[0]):
            copy.start()

    def hand_on(k):
        for copy in out_z(k):
            copy.wait_recv()
        for copy in out_y(k)[1:]:
            copy.start()

    def after_all(k):
        for copy in out_z(k):
            copy.wait_send()
        for copy in out_y(k):
            copy.wait()
        layer, c = 1 - k // CHUNKS, k % CHUNKS
        for q in range(2):
            for n, (out, half) in enumerate(((og_ref, 0), (og_ref, CHUNKS), (ou_ref, 0), (ou_ref, CHUNKS))):
                src = fin.at[k, 96 * q : 96 * q + 64, 128 * n : 128 * n + 128]
                dst = out.at[layer, 64 * q : 64 * q + 64, lanes(c + half)]
                pltpu.make_async_copy(src, dst, osem.at[layer, n // 2]).start()

    def when(cond, f, k):
        pl.when(cond)(lambda: f(k))

    def into(layer, t, n):
        at = pl.ds(pl.multiple_of(t * n, n), n)
        by_a = nt(DGU[0, at, :], W[layer, 0])
        for c in range(1, CHUNKS):
            by_a += nt(DGU[c, at, :], W[layer, c])
        by_a = by_a.astype(BF).astype(F32)
        wide = XH[at, :].astype(F32)
        scale = scale_of(wide)
        back = by_a * scale - wide * (scale * scale * scale * jnp.mean(by_a * wide, -1, keepdims=True))
        G[at, :] = (G[at, :].astype(F32) + back.astype(BF).astype(F32)).astype(BF)

    load_a = pltpu.make_async_copy(dx_ref, A, asem.at[4])

    def step(k, carry):
        layer, c = 1 - k // CHUNKS, k % CHUNKS

        @pl.when(k == CHUNKS)
        def _():
            load_a.start()

            def one(t, carry):
                into(1, t, tt)
                return carry

            lax.fori_loop(0, 4, one, 0)
            for copy in load_x:
                copy.start()
            load_a.wait()

        @pl.when(k < CHUNKS)
        def _():
            @pl.when(k + 3 < CHUNKS)
            def _():
                pass_x(1, k + 3)

            @pl.when(k + 1 < CHUNKS)
            def _():
                pass_y(1, k + 1)

            arrived(1, k)

        rows = pl.ds(pl.multiple_of(256 * c, 256), 256)

        def front(t):
            gu = nn(A[tile[t], :], W[layer, c])
            gate, up = gu[:, 0:256], gu[:, 256:512]
            by_act = nt(G[tile[t], :], WD[layer, rows, :]).astype(BF).astype(F32)
            sig, silu = gated(gate)
            AC2[t % 2] = (silu * up).astype(BF)
            DGU[c, tile[t], 0:256] = (by_act * up * (sig * (1.0 + (gate - silu)))).astype(BF)
            DGU[c, tile[t], 256:512] = (by_act * silu).astype(BF)

        def back(t):
            gu, dn = tn(A[tile[t], :], DGU[c, tile[t], :]), tn(AC2[t % 2], G[tile[t], :])
            ACC[...] = ACC[...] + gu if t else gu
            ACD[...] = ACD[...] + dn if t else dn

        front(0)
        front(1)
        back(0)
        when(k >= 2, after_x, k - 2)
        when(k >= 1, after_core, k - 1)
        front(2)
        back(1)
        front(3)
        back(2)
        back(3)
        when(k >= 5, after_all, k - 5)
        when(k >= 4, hand_on, k - 4)
        when(k >= 3, after_z, k - 3)
        when(k >= 2, after_y, k - 2)
        send_core()
        core_copy(k).start()
        return carry

    lax.fori_loop(0, STEPS, step, 0)

    last = STEPS - 1
    e = tokens // 8
    eighth = [pl.ds(i * e, e) for i in range(8)]
    store_dx = [pltpu.make_async_copy(G.at[t, :], dx_ref.at[t, :], asem.at[i]) for i, t in enumerate(eighth)]

    def by_x(i):
        into(0, i, e)
        store_dx[i].start()

    def down_copies(layer):
        first = (1 - layer) * CHUNKS + (CHUNKS - 2) * (1 - core)
        return [
            remote(fin.at[pl.ds(first, 2), 96 * q + 64 : 96 * q + 96, :], dnx.at[layer, :, 32 * q : 32 * q + 32, :], dns.at[layer, q], dnr.at[layer, q], partner)
            for q in range(2)
        ]

    def put_down(layer):
        for copy in down_copies(layer):
            copy.wait()
        copies = []
        for n in range(3):
            for q in range(2):
                src = fin.at[(1 - layer) * CHUNKS + n + 2 * core, 96 * q + 64 : 96 * q + 96, :]
                copies.append((src, od_ref.at[layer, 128 * n + 32 * q : 128 * n + 32 * q + 32, :]))
        for n in range(2):
            copies.append((dnx.at[layer, n], od_ref.at[layer, 128 * n + 64 : 128 * n + 128, :]))
        for src, dst in copies:
            pltpu.make_async_copy(src, dst, osem.at[layer, 2]).start()

    for copy in load_x:
        copy.wait()
    for copy in down_copies(1):
        copy.start()
    after_x(last - 1)
    by_x(0)
    after_core(last)
    after_z(last - 2)
    hand_on(last - 3)
    by_x(1)
    after_y(last - 1)
    after_all(last - 4)
    by_x(2)
    by_x(3)
    hand_on(last - 2)
    after_all(last - 3)
    after_x(last)
    by_x(4)
    after_z(last - 1)
    by_x(5)
    after_y(last)
    put_down(1)
    by_x(6)
    hand_on(last - 1)
    after_all(last - 2)
    by_x(7)
    after_z(last)
    after_all(last - 1)
    for layer in range(2):
        for row in range(5):
            for p in range(CHUNKS + 5):
                fetch(layer, p, KINDS[row]).wait_send()
    hand_on(last)
    after_all(last)
    for copy in down_copies(0):
        copy.start()
    put_down(0)
    for copy in store_dx:
        copy.wait()
    for layer in range(2):
        for n, out in enumerate((og_ref, ou_ref, od_ref)):
            pltpu.make_async_copy(out.at[layer], out.at[layer], osem.at[layer, n]).wait()


def place_results(*refs):
    sources, results, held, (rsem, wsem) = refs[:4], refs[4:8], refs[8:12], refs[12:]
    n = sources[0].shape[0] // 8
    cuts = [(0, pl.ds(i * n, n)) for i in range(8)] + [(j, layer) for j in range(1, 4) for layer in range(LAYERS)]
    reads = [pltpu.make_async_copy(sources[j].at[at], held[j].at[at], rsem.at[i]) for i, (j, at) in enumerate(cuts)]
    writes = [pltpu.make_async_copy(held[j].at[at], results[j].at[at], wsem.at[i]) for i, (j, at) in enumerate(cuts)]
    for copy in reads:
        copy.start()
    for read, write in zip(reads, writes, strict=True):
        read.wait()
        write.start()
    for copy in writes:
        copy.wait()


def solution(mesh):
    def step(x, dy, wg, wu, wd):
        tokens = x.shape[1]
        tt = tokens // 4
        hbm = pl.BlockSpec(memory_space=pl.ANY)
        V, DMA = pltpu.VMEM, pltpu.SemaphoreType.DMA
        dx, *grads = pl.pallas_call(
            kernel,
            out_shape=[
                jax.ShapeDtypeStruct((tokens, D), BF),
                *(jax.ShapeDtypeStruct(w.shape, BF) for w in (wg, wu, wd)),
            ],
            in_specs=[hbm] * 5,
            out_specs=[hbm] * 4,
            scratch_shapes=[
                V((LAYERS, CHUNKS, D, 512), BF), V((LAYERS, FF, D), BF),
                V((tokens, D), BF), V((tokens, D), BF), V((tokens, D), BF), V((CHUNKS, tokens, 512), BF),
                V((D, 512), F32), V((256, D), F32), V((2, tt, 256), BF),
                V((2, 192, 512), F32), V((2, 192, 512), BF), V((2, 2, 192, 512), BF),
                V((192, 512), F32), V((192, 512), BF), V((2, 192, 512), BF),
                V((96, 512), F32), V((96, 512), BF), V((2, 96, 512), BF),
                V((96, 512), F32), V((96, 512), BF), V((2, 3, 96, 128), BF),
                V((STEPS, 192, 512), BF), V((LAYERS, 2, 64, 512), BF),
                DMA((LAYERS, CHUNKS, 4)), DMA((LAYERS, 5)), DMA((5,)), DMA((8,)), DMA((LAYERS, 3)),
                DMA((LAYERS, 5, CHUNKS + 5)), DMA((LAYERS, 5, CHUNKS + 5)), DMA((4, 2)), DMA((4, 2)),
                DMA((2, 3)), DMA((2, 3)), DMA((4, 3)), DMA((4, 3)), DMA((4, 4)), DMA((4, 4)), DMA((2, 2)), DMA((2, 2)),
            ],
            compiler_params=pltpu.CompilerParams(collective_id=0, has_side_effects=True, vmem_limit_bytes=67_043_328),
        )(x[0], dy[0], wg, wu, wd)
        V, DMA = pltpu.VMEM, pltpu.SemaphoreType.DMA
        results = (dx, *grads)
        dx, *grads = pl.pallas_call(
            place_results,
            out_shape=[jax.ShapeDtypeStruct(a.shape, BF) for a in results],
            in_specs=[hbm] * 4,
            out_specs=[hbm] * 4,
            scratch_shapes=[*(V(a.shape, BF) for a in results), DMA((14,)), DMA((14,))],
            compiler_params=pltpu.CompilerParams(vmem_limit_bytes=60_000_000),
        )(*results)
        return (dx[None], *grads)

    states, cut = P(("rep", "r", "s"), None, None), P(None, "s", None)
    return jax.shard_map(
        step,
        mesh=mesh,
        in_specs=(states, states) + (cut,) * 3,
        out_specs=(states,) + (P("rep", "s", None),) * 3,
        check_vma=False,
    )
```

time: 195 us -> 173 us (0.89)
  Pallas kernels: 187 us -> 172 us
  local copies, waits for them, and re-layouts: 7.13 us -> 0 us
    pallas_call x1, Pallas kernels: 187 us -> 166 us  [step(): pl.pallas_call(kernel, out_shape=[jax.ShapeDtypeStruct((tokens, D), BF),...]
    unnamed x10 -> x0, local copies, waits for them, and re-layouts: 7.13 us -> none
    pallas_call x0 -> x1, Pallas kernels: none -> 5.42 us  [step(): pl.pallas_call(place_results, out_shape=[jax.ShapeDtypeStruct(a.shape, BF...]
where the time goes in v2:
time: 173 us; the launch traced here: 172 us
  Pallas kernels  172 us (99%)
    pallas_call x1, Pallas kernels, step(): pl.pallas_call(kernel, out_shape=[jax.ShapeDtypeStruct((tokens, D), BF),...  166 us
    pallas_call x1, Pallas kernels, step(): pl.pallas_call(place_results, out_shape=[jax.ShapeDtypeStruct(a.shape, BF...  5.42 us

profile of v2, /device:TPU:0, one launch (start us, length us, event | category | flops | bytes accessed | tf_op | source)
XLA Modules:
  0.0 172.4 jit_solution(15591302150941882216)
XLA Ops:
  0.6 166.2 %shard_map.84 = (bf16[4096,512]{1,0:T(8,128)(2,1)}, bf16[2,128,1280]{2,1,0:T(8,128)(2,1)}, bf16[2,128,1280]{2,1,0:T(8,128)(2,1)}, bf16[2,320,512]{2,1,0:T(8,128)(2,1)}) custom-call(bf16[4096,512]{1,0:T(8,128)(2,1)} %bitcast.3, bf16[4096,512]{1,0:T(8,128)(2,1)} %bitcast.4, bf16[2,128,1280]{2,1,0:T(8,128)(2,1)} %wg_ref.1, bf16[2,128,1280]{2,1,0:T(8,128)(2,1)} %wu_ref.1, ...), custom_call_target="tpu_custom_call" | custom-call | tf_op jit(solution)/shard_map/pallas_call | solution.py:471
  166.8 5.4 %shard_map.85 = (bf16[4096,512]{1,0:T(8,128)(2,1)}, bf16[2,128,1280]{2,1,0:T(8,128)(2,1)}, bf16[2,128,1280]{2,1,0:T(8,128)(2,1)}, bf16[2,320,512]{2,1,0:T(8,128)(2,1)}) custom-call(bf16[4096,512]{1,0:T(8,128)(2,1)} %get-tuple-element.12.refs_0_, bf16[2,128,1280]{2,1,0:T(8,128)(2,1)} %get-tuple-element.13.refs_1_, ...), custom_call_target="tpu_custom_call" | custom-call | tf_op jit(solution)/shard_map/pallas_call | solution.py:496

commit v3 on v2

--- a/solution.py
+++ b/solution.py
@@ -38,10 +38,10 @@
 
 def kernel(
     x_ref, dy_ref, wg_ref, wu_ref, wd_ref,
-    dx_ref, og_ref, ou_ref, od_ref,
-    W, WD, XH, A, G, DGU, ACC, ACD, AC2,
-    S0, s0s, s0r, S1, s1s, s1r, S2, s2s, s2r, S3, s3s, s3r, fin, dnx,
-    lsem, ldsem, xsem, asem, osem, gss, grs, ss, rs, zs, zr, azs, azr, ays, ayr, dns, dnr,
+    G, og_ref, ou_ref, od_ref, a_ref,
+    W, WD, XH, A, DGU, ACC, ACD, AC2,
+    S0, s0s, s0r, S1, s1s, s1r, S2, s2s, s2r, S3, s3s, s3r, near8, fin, dnx,
+    lsem, ldsem, xsem, asem, gss, grs, ss, rs, zs, zr, azs, azr, ays, ayr, dns, dnr, n8s, n8r, a8s, a8r,
 ):
     r, s = lax.axis_index("r"), lax.axis_index("s")
     y, z = r // 4, r % 4
@@ -138,7 +138,7 @@
     downs = range(CHUNKS, CHUNKS + 5)
     for p in range(CHUNKS + 5):
         begin(0, p)
-    save_a = [pltpu.make_async_copy(A.at[t, :], dx_ref.at[t, :], asem.at[i]) for i, t in enumerate(tile)]
+    save_a = [pltpu.make_async_copy(A.at[t, :], a_ref.at[t, :], asem.at[i]) for i, t in enumerate(tile)]
     for t in range(4):
         load_x[t].wait()
         wide = XH[tile[t], :].astype(F32)
@@ -222,7 +222,7 @@
 
     def z_copies(k):
         return [
-            remote(s3s.at[:, lanes((z + j) % 4)], s3r.at[k % 2, j - 1], zs.at[k % 2, j - 1], zr.at[k % 2, j - 1], place(0, j)) for j in range(1, 4)
+            remote(s3s.at[k % 2, :, lanes((z + j) % 4)], s3r.at[k % 2, j - 1], zs.at[k % 2, j - 1], zr.at[k % 2, j - 1], place(0, j)) for j in range(1, 4)
         ]
 
     def piece(k, z_=z):
@@ -261,20 +261,51 @@
 
     def after_y(k):
         y_copy(k).wait()
-        S3[...] = S2[...] + s2r[k % 2].astype(F32)
-        s3s[...] = S3[...].astype(BF)
+        S2[...] += s2r[k % 2].astype(F32)
+        s3s[k % 2] = S2[...].astype(BF)
         for copy in z_copies(k):
             copy.start()
+        S3[k % 2] = S2[:, lanes(z)]
 
     def after_z(k):
         for copy in z_copies(k):
             copy.wait()
-        total = S3[:, lanes(z)]
-        for j in range(3):
-            total += s3r[k % 2, j].astype(F32)
+        send_out(k, [s3r[k % 2, j] for j in range(3)], lambda k: (*out_z(k), out_y(k)[0]))
+
+    def send_out(k, terms, copies):
+        total = S3[k % 2]
+        for term in terms:
+            total += term.astype(F32)
         piece(k)[...] = total.astype(BF)
-        for copy in (*out_z(k), out_y(k)[0]):
+        for copy in copies(k):
             copy.start()
+
+    def out_all(k):
+        return [remote(piece(k), piece(k), a8s.at[i], a8r.at[i], place(*o)) for i, o in enumerate(others)]
+
+    def to_all(src, dy_, dzs):
+        return [remote(src.at[:, lanes((z + j) % 4)], near8.at[4 * dy_ + j - 1], n8s.at[4 * dy_ + j - 1], n8r.at[4 * dy_ + j - 1], place(dy_, j)) for j in dzs]
+
+    def last_over_y(k):
+        x_copies(k)[0].wait()
+        give = some(96 * (1 - y), 96)
+        s2s[...] = (S1[give, :] + s1r[k % 2, give, :].astype(F32)).astype(BF)
+        for copy in to_all(s2s, 1, range(4)):
+            copy.start()
+
+    def last_over_z(k):
+        x_copies(k)[1].wait()
+        keep = some(96 * y, 96)
+        S2[...] = S1[keep, :] + s1r[k % 2, keep, :].astype(F32)
+        s3s[k % 2] = S2[...].astype(BF)
+        for copy in to_all(s3s.at[k % 2], 0, range(1, 4)):
+            copy.start()
+        S3[k % 2] = S2[:, lanes(z)]
+
+    def last_sum(k):
+        for copy in (*to_all(s2s, 1, range(4)), *to_all(s3s.at[k % 2], 0, range(1, 4))):
+            copy.wait()
+        send_out(k, [near8[j] for j in range(7)], out_all)
 
     def hand_on(k):
         for copy in out_z(k):
@@ -287,12 +318,13 @@
             copy.wait_send()
         for copy in out_y(k):
             copy.wait()
+        put_chunk(k)
+
+    def put_chunk(k):
         layer, c = 1 - k // CHUNKS, k % CHUNKS
         for q in range(2):
             for n, (out, half) in enumerate(((og_ref, 0), (og_ref, CHUNKS), (ou_ref, 0), (ou_ref, CHUNKS))):
-                src = fin.at[k, 96 * q : 96 * q + 64, 128 * n : 128 * n + 128]
-                dst = out.at[layer, 64 * q : 64 * q + 64, lanes(c + half)]
-                pltpu.make_async_copy(src, dst, osem.at[layer, n // 2]).start()
+                out[layer, 64 * q : 64 * q + 64, lanes(c + half)] = fin[k, 96 * q : 96 * q + 64, 128 * n : 128 * n + 128]
 
     def when(cond, f, k):
         pl.when(cond)(lambda: f(k))
@@ -308,7 +340,9 @@
         back = by_a * scale - wide * (scale * scale * scale * jnp.mean(by_a * wide, -1, keepdims=True))
         G[at, :] = (G[at, :].astype(F32) + back.astype(BF).astype(F32)).astype(BF)
 
-    load_a = pltpu.make_async_copy(dx_ref, A, asem.at[4])
+    load_a = pltpu.make_async_copy(a_ref, A, asem.at[4])
+
+    e = tokens // 8
 
     def step(k, carry):
         layer, c = 1 - k // CHUNKS, k % CHUNKS
@@ -318,7 +352,8 @@
             load_a.start()
 
             def one(t, carry):
-                into(1, t, tt)
+                into(1, 2 * t, e)
+                into(1, 2 * t + 1, e)
                 return carry
 
             lax.fori_loop(0, 4, one, 0)
@@ -375,13 +410,8 @@
     lax.fori_loop(0, STEPS, step, 0)
 
     last = STEPS - 1
-    e = tokens // 8
-    eighth = [pl.ds(i * e, e) for i in range(8)]
-    store_dx = [pltpu.make_async_copy(G.at[t, :], dx_ref.at[t, :], asem.at[i]) for i, t in enumerate(eighth)]
-
     def by_x(i):
         into(0, i, e)
-        store_dx[i].start()
 
     def down_copies(layer):
         first = (1 - layer) * CHUNKS + (CHUNKS - 2) * (1 - core)
@@ -393,72 +423,58 @@
     def put_down(layer):
         for copy in down_copies(layer):
             copy.wait()
-        copies = []
         for n in range(3):
             for q in range(2):
-                src = fin.at[(1 - layer) * CHUNKS + n + 2 * core, 96 * q + 64 : 96 * q + 96, :]
-                copies.append((src, od_ref.at[layer, 128 * n + 32 * q : 128 * n + 32 * q + 32, :]))
+                block = fin[(1 - layer) * CHUNKS + n + 2 * core, 96 * q + 64 : 96 * q + 96, :]
+                od_ref[layer, 128 * n + 32 * q : 128 * n + 32 * q + 32, :] = block
         for n in range(2):
-            copies.append((dnx.at[layer, n], od_ref.at[layer, 128 * n + 64 : 128 * n + 128, :]))
-        for src, dst in copies:
-            pltpu.make_async_copy(src, dst, osem.at[layer, 2]).start()
+            od_ref[layer, 128 * n + 64 : 128 * n + 128, :] = dnx[layer, n]
 
     for copy in load_x:
         copy.wait()
     for copy in down_copies(1):
         copy.start()
+    by_x(0)
     after_x(last - 1)
-    by_x(0)
     after_core(last)
+    by_x(1)
+    after_all(last - 4)
+    hand_on(last - 3)
+    by_x(2)
     after_z(last - 2)
-    hand_on(last - 3)
-    by_x(1)
     after_y(last - 1)
-    after_all(last - 4)
-    by_x(2)
+    last_over_y(last)
     by_x(3)
+    last_over_z(last)
+    by_x(4)
     hand_on(last - 2)
     after_all(last - 3)
-    after_x(last)
-    by_x(4)
+    by_x(5)
     after_z(last - 1)
-    by_x(5)
-    after_y(last)
+    by_x(6)
+    last_sum(last)
+    by_x(7)
     put_down(1)
-    by_x(6)
     hand_on(last - 1)
     after_all(last - 2)
-    by_x(7)
-    after_z(last)
-    after_all(last - 1)
     for layer in range(2):
         for row in range(5):
             for p in range(CHUNKS + 5):
                 fetch(layer, p, KINDS[row]).wait_send()
-    hand_on(last)
-    after_all(last)
+    after_all(last - 1)
+    for copy in out_all(last):
+        copy.wait()
+    put_chunk(last)
     for copy in down_copies(0):
         copy.start()
     put_down(0)
-    for copy in store_dx:
-        copy.wait()
-    for layer in range(2):
-        for n, out in enumerate((og_ref, ou_ref, od_ref)):
-            pltpu.make_async_copy(out.at[layer], out.at[layer], osem.at[layer, n]).wait()
 
 
 def place_results(*refs):
-    sources, results, held, (rsem, wsem) = refs[:4], refs[4:8], refs[8:12], refs[12:]
-    n = sources[0].shape[0] // 8
-    cuts = [(0, pl.ds(i * n, n)) for i in range(8)] + [(j, layer) for j in range(1, 4) for layer in range(LAYERS)]
-    reads = [pltpu.make_async_copy(sources[j].at[at], held[j].at[at], rsem.at[i]) for i, (j, at) in enumerate(cuts)]
-    writes = [pltpu.make_async_copy(held[j].at[at], results[j].at[at], wsem.at[i]) for i, (j, at) in enumerate(cuts)]
-    for copy in reads:
+    copies = [pltpu.make_async_copy(refs[i], refs[4 + i], refs[8].at[i]) for i in range(4)]
+    for copy in copies:
         copy.start()
-    for read, write in zip(reads, writes, strict=True):
-        read.wait()
-        write.start()
-    for copy in writes:
+    for copy in copies:
         copy.wait()
 
 
@@ -466,40 +482,41 @@
     def step(x, dy, wg, wu, wd):
         tokens = x.shape[1]
         tt = tokens // 4
-        hbm = pl.BlockSpec(memory_space=pl.ANY)
+        hbm, vmem = pl.BlockSpec(memory_space=pl.ANY), pl.BlockSpec(memory_space=pltpu.VMEM)
         V, DMA = pltpu.VMEM, pltpu.SemaphoreType.DMA
-        dx, *grads = pl.pallas_call(
+        dx, *grads, _ = pl.pallas_call(
             kernel,
             out_shape=[
+                V((tokens, D), BF),
+                *(V(w.shape, BF) for w in (wg, wu, wd)),
                 jax.ShapeDtypeStruct((tokens, D), BF),
-                *(jax.ShapeDtypeStruct(w.shape, BF) for w in (wg, wu, wd)),
             ],
             in_specs=[hbm] * 5,
-            out_specs=[hbm] * 4,
+            out_specs=[vmem] * 4 + [hbm],
             scratch_shapes=[
                 V((LAYERS, CHUNKS, D, 512), BF), V((LAYERS, FF, D), BF),
-                V((tokens, D), BF), V((tokens, D), BF), V((tokens, D), BF), V((CHUNKS, tokens, 512), BF),
+                V((tokens, D), BF), V((tokens, D), BF), V((CHUNKS, tokens, 512), BF),
                 V((D, 512), F32), V((256, D), F32), V((2, tt, 256), BF),
                 V((2, 192, 512), F32), V((2, 192, 512), BF), V((2, 2, 192, 512), BF),
                 V((192, 512), F32), V((192, 512), BF), V((2, 192, 512), BF),
                 V((96, 512), F32), V((96, 512), BF), V((2, 96, 512), BF),
-                V((96, 512), F32), V((96, 512), BF), V((2, 3, 96, 128), BF),
+                V((2, 96, 128), F32), V((2, 96, 512), BF), V((2, 3, 96, 128), BF), V((7, 96, 128), BF),
                 V((STEPS, 192, 512), BF), V((LAYERS, 2, 64, 512), BF),
-                DMA((LAYERS, CHUNKS, 4)), DMA((LAYERS, 5)), DMA((5,)), DMA((8,)), DMA((LAYERS, 3)),
+                DMA((LAYERS, CHUNKS, 4)), DMA((LAYERS, 5)), DMA((5,)), DMA((5,)),
                 DMA((LAYERS, 5, CHUNKS + 5)), DMA((LAYERS, 5, CHUNKS + 5)), DMA((4, 2)), DMA((4, 2)),
-                DMA((2, 3)), DMA((2, 3)), DMA((4, 3)), DMA((4, 3)), DMA((4, 4)), DMA((4, 4)), DMA((2, 2)), DMA((2, 2)),
+                DMA((2, 3)), DMA((2, 3)), DMA((4, 3)), DMA((4, 3)), DMA((4, 4)), DMA((4, 4)), DMA((2, 2)), DMA((2, 2)), DMA((7,)), DMA((7,)), DMA((7,)), DMA((7,)),
             ],
-            compiler_params=pltpu.CompilerParams(collective_id=0, has_side_effects=True, vmem_limit_bytes=67_043_328),
+            compiler_params=pltpu.CompilerParams(collective_id=0, has_side_effects=True, vmem_limit_bytes=60_500_000),
         )(x[0], dy[0], wg, wu, wd)
         V, DMA = pltpu.VMEM, pltpu.SemaphoreType.DMA
         results = (dx, *grads)
         dx, *grads = pl.pallas_call(
             place_results,
             out_shape=[jax.ShapeDtypeStruct(a.shape, BF) for a in results],
-            in_specs=[hbm] * 4,
+            in_specs=[vmem] * 4,
             out_specs=[hbm] * 4,
-            scratch_shapes=[*(V(a.shape, BF) for a in results), DMA((14,)), DMA((14,))],
-            compiler_params=pltpu.CompilerParams(vmem_limit_bytes=60_000_000),
+            scratch_shapes=[DMA((4,))],
+            compiler_params=pltpu.CompilerParams(vmem_limit_bytes=16_000_000),
         )(*results)
         return (dx[None], *grads)
 

time: 173 us -> 168 us (0.971)
  Pallas kernels: 172 us -> 167 us
    pallas_call x1, Pallas kernels: 5.42 us -> 2.65 us  [step(): pl.pallas_call(place_results, out_shape=[jax.ShapeDtypeStruct(a.shape, BF...]
where the time goes in v3:
time: 168 us
  Pallas kernels  167 us (99%)
    pallas_call x1, Pallas kernels, step(): pl.pallas_call(kernel, out_shape=[V((tokens, D), BF), *(V(w.shape, BF) fo...  165 us

profile of v3, /device:TPU:0, one launch (start us, length us, event | category | flops | bytes accessed | tf_op | source)
XLA Modules:
  0.0 168.2 jit_solution(16721643722791088219)
XLA Ops:
  0.6 164.7 %shard_map.84 = (bf16[4096,512]{1,0:T(8,128)(2,1)S(1)}, bf16[2,128,1280]{2,1,0:T(8,128)(2,1)S(1)}, bf16[2,128,1280]{2,1,0:T(8,128)(2,1)S(1)}, bf16[2,320,512]{2,1,0:T(8,128)(2,1)S(1)}, bf16[4096,512]{1,0:T(8,128)(2,1)}) custom-call(bf16[4096,512]{1,0:T(8,128)(2,1)} %bitcast.3, bf16[4096,512]{1,0:T(8,128)(2,1)} %bitcast.4, bf16[2,128,1280]{2,1,0:T(8,128)(2,1)} %wg_ref.1, ...), custom_call_target="tpu_custom_call" | custom-call | tf_op jit(solution)/shard_map/pallas_call | solution.py:487
  165.3 2.6 %shard_map.85 = (bf16[4096,512]{1,0:T(8,128)(2,1)}, bf16[2,128,1280]{2,1,0:T(8,128)(2,1)}, bf16[2,128,1280]{2,1,0:T(8,128)(2,1)}, bf16[2,320,512]{2,1,0:T(8,128)(2,1)}) custom-call(bf16[4096,512]{1,0:T(8,128)(2,1)S(1)} %get-tuple-element.12.refs_0_, bf16[2,128,1280]{2,1,0:T(8,128)(2,1)S(1)} %get-tuple-element.13.refs_1_, ...), custom_call_target="tpu_custom_call" | custom-call | tf_op jit(solution)/shard_map/pallas_call | solution.py:513
